TPU v7x, 32 devices: a whole 2x2x4 slice. The times are simulated.
32 devices in a mesh: bank: 4 (over x, core), zero: 8 (over z, y).
Axes of the slice: x: 2, y: 2, z: 4, core: 2. Of those that a mesh axis runs over, the one named last changes fastest.
Arguments:
- train_gate: float32 [128, 2048, 768], P('bank', 'zero'), may hold values from -0.1875 to 0.1875
- other_gate: bfloat16 [128, 2048, 768], P('bank', 'zero'), may hold values from -0.0625 to 0.0625
- train_up: float32 [128, 2048, 768], P('bank', 'zero'), may hold values from -0.1875 to 0.1875
- other_up: bfloat16 [128, 2048, 768], P('bank', 'zero'), may hold values from -0.0625 to 0.0625
- router_weight: float32 [2048, 128], P('zero', 'bank'), may hold values from -0.125 to 0.125
- router_gain: float32 [2048], P('zero'), may hold values from 0.25 to 1.75
Outputs:
- ready_gate: bfloat16 [128, 2048, 768], P('bank', None, 'zero')
- ready_up: bfloat16 [128, 2048, 768], P('bank', None, 'zero')
- scale_gate: float32 [128, 768], P('bank', 'zero')
- scale_up: float32 [128, 768], P('bank', 'zero')
- serve_router: bfloat16 [2048, 128], replicated
All inputs are finite; a program needn't handle non-finite values. Where the computation divides by a largest or mean magnitude, that divisor is 1e-20 or more.
Results may differ from a plain program's by a relative error of at most 0.001.
Values may be sent and summed in bfloat16 or wider, within the bound.
No kernel may reach another device: no remote copies, remote signals or barrier semaphores. Data moves between devices by JAX's collectives and lax.ppermute only.
A program may use at most 256 MiB of HBM per device.

v0:
```python
import jax
import jax.numpy as jnp
from jax import lax
from jax.sharding import PartitionSpec as P


def on_device(train_gate, other_gate, train_up, other_up, router_weight, router_gain):
    latest_gate = train_gate + other_gate.astype(jnp.float32)
    latest_up = train_up + other_up.astype(jnp.float32)
    scale_gate, scale_up = lax.pmax(
        (jnp.max(jnp.abs(latest_gate), axis=1), jnp.max(jnp.abs(latest_up), axis=1)), "zero"
    )
    narrow_gate, narrow_up = (
        (latest_gate / jnp.expand_dims(scale_gate, 1)).astype(jnp.bfloat16),
        (latest_up / jnp.expand_dims(scale_up, 1)).astype(jnp.bfloat16),
    )
    ready_gate, ready_up = (
        lax.all_to_all(narrow_gate, "zero", split_axis=2, concat_axis=1, tiled=True),
        lax.all_to_all(narrow_up, "zero", split_axis=2, concat_axis=1, tiled=True),
    )
    scale_gate = lax.dynamic_slice_in_dim(
        scale_gate, lax.axis_index("zero") * ready_gate.shape[2], ready_gate.shape[2], axis=1
    )
    scale_up = lax.dynamic_slice_in_dim(
        scale_up, lax.axis_index("zero") * ready_up.shape[2], ready_up.shape[2], axis=1
    )
    part_router = (router_weight * router_gain[:, None]).astype(jnp.bfloat16)
    row_router = lax.all_gather(part_router, "zero", axis=0, tiled=True)
    serve_router = lax.all_gather(row_router, "bank", axis=1, tiled=True)
    return (ready_gate, ready_up, scale_gate, scale_up, serve_router)


def solution(mesh):
    return jax.shard_map(
        on_device,
        mesh=mesh,
        in_specs=(
            P("bank", "zero", None),
            P("bank", "zero", None),
            P("bank", "zero", None),
            P("bank", "zero", None),
            P("zero", "bank"),
            P("zero"),
        ),
        out_specs=(
            P("bank", None, "zero"),
            P("bank", None, "zero"),
            P("bank", "zero"),
            P("bank", "zero"),
            P(),
        ),
        check_vma=False,
    )
```

profile of v0, /device:TPU:0, one launch (start us, length us, event | category | flops | bytes accessed | tf_op | source)
XLA Modules:
  0.0 885.5 jit_solution(4941322030642369728)
XLA Ops:
  7.2 0.0 all-reduce.3.cloned.1.call-start
  7.2 25.0 %copy.42 = f32[32,256,768]{1,0,2:T(8,128)} copy(f32[32,256,768]{2,1,0:T(8,128)} %param.8) | data formatting | bytes 50331648 | tf_op args[2]
  32.2 16.9 %copy.41 = bf16[32,256,768]{1,0,2:T(8,128)(2,1)} copy(bf16[32,256,768]{2,1,0:T(8,128)(2,1)} %param.9) | data formatting | bytes 25165824 | tf_op args[3]
  49.1 25.0 %copy.38 = f32[32,256,768]{1,0,2:T(8,128)} copy(f32[32,256,768]{2,1,0:T(8,128)} %param.6) | data formatting | bytes 50331648 | tf_op args[0]
  74.2 16.9 %copy.37 = bf16[32,256,768]{1,0,2:T(8,128)(2,1)} copy(bf16[32,256,768]{2,1,0:T(8,128)(2,1)} %param.7) | data formatting | bytes 25165824 | tf_op args[1]
  91.0 0.0 copy-start
  91.0 14.4 %abs_reduce_fusion = f32[32,768]{0,1:T(8,128)} fusion(f32[32,256,768]{1,0,2:T(8,128)} %copy.42, bf16[32,256,768]{1,0,2:T(8,128)(2,1)} %copy.41), kind=kLoop, calls=%fused_computation.1 | loop fusion | flops 25141248 | bytes 37847040 | tf_op jit(solution)/shard_map/reduce_max | solution.py:11
  105.4 4.7 copy-done
  110.1 9.7 %abs_reduce_fusion.1 = f32[32,768]{0,1:T(8,128)} fusion(f32[32,256,768]{1,0,2:T(8,128)S(1)} %copy-done, bf16[32,256,768]{1,0,2:T(8,128)(2,1)} %copy.37), kind=kLoop, calls=%fused_computation.4 | loop fusion | flops 25141248 | bytes 37847040 | tf_op jit(solution)/shard_map/reduce_max | solution.py:11
  119.9 0.0 all-reduce.3.cloned.1.call-update
  119.9 78.2 %all-reduce.3.cloned.1.call-done = (f32[32,768]{0,1:T(8,128)}, f32[32,768]{0,1:T(8,128)}) async-done(((f32[32,768]{0,1:T(8,128)}, f32[32,768]{0,1:T(8,128)}), (f32[32,768]{0,1:T(8,128)}, f32[32,768]{0,1:T(8,128)})) %all-reduce.3.cloned.1.call-update) | async-done | bytes 196624 | tf_op jit(solution)/shard_map/pmax | solution.py:10
  198.1 29.4 %divide_convert_fusion = (bf16[32,256,768]{1,0,2:T(8,128)(2,1)}, bf16[32,256,768]{1,0,2:T(8,128)(2,1)S(1)}) fusion(f32[32,256,768]{1,0,2:T(8,128)} %copy.42, bf16[32,256,768]{1,0,2:T(8,128)(2,1)} %copy.41, f32[32,768]{0,1:T(8,128)} %get-tuple-element.16, f32[32,768]{0,1:T(8,128)} %get-tuple-element.15, f32[32,256,768]{1,0,2:T(8,128)} %copy.38, ...), kind=kLoop, calls=%fused_computation | loop fusion | flops 50331648 | bytes 100859904 | tf_op jit(solution)/shard_map/convert_element_type | solution.py:15
  227.5 0.0 copy-start.1
  227.6 0.0 copy-start.2
  227.6 276.4 %all_to_all.36 = bf16[32,256,768]{1,0,2:T(8,128)(2,1)} all-to-all(bf16[32,256,768]{1,0,2:T(8,128)(2,1)S(1)} %get-tuple-element.18), channel_id=1, replica_groups=mesh['bank'=4,'zero'=8] {'zero'}, dimensions={2} | all-to-all | bytes 25165824 | tf_op jit(solution)/shard_map/all_to_all | solution.py:18
  504.0 5.4 all-to-all-start.1
  509.3 0.0 copy-done.1
  509.4 0.0 copy-done.2
  509.4 292.0 %all_gather.6 = bf16[2048,32]{0,1:T(8,128)(2,1)S(1)} all-gather(bf16[256,32]{0,1:T(8,128)(2,1)S(1)} %multiply_convert_fusion), channel_id=1, replica_groups=mesh['bank'=4,'zero'=8] {'zero'}, dimensions={0}, use_global_device_ids=true | all-gather | bytes 147456 | tf_op jit(solution)/shard_map/all_gather | solution.py:28
  801.4 7.0 all_gather.7
  808.4 1.0 copy.47
  809.4 0.8 constant_dynamic-slice_fusion
  810.2 0.7 copy.45
  810.9 0.7 copy.46
  811.6 14.1 %copy.40 = bf16[32,8,256,96]{2,1,3,0:T(8,128)(2,1)} copy(bf16[32,8,256,96]{2,0,3,1:T(8,128)(2,1)} %bitcast.14) | data formatting | bytes 25165824 | tf_op jit(solution)/shard_map/all_to_all | solution.py:18
  825.6 19.5 %all_to_all.29 = bf16[32,2048,96]{1,2,0:T(8,128)(2,1)} reshape(bf16[32,8,256,96]{2,1,3,0:T(8,128)(2,1)} %copy.40) | data formatting | bytes 25165824 | tf_op jit(solution)/shard_map/all_to_all | solution.py:18
  845.1 0.0 all-to-all-done.1
  845.1 14.1 %copy.44 = bf16[32,8,256,96]{2,1,3,0:T(8,128)(2,1)} copy(bf16[32,8,256,96]{2,0,3,1:T(8,128)(2,1)} %bitcast.5) | data formatting | bytes 25165824 | tf_op jit(solution)/shard_map/all_to_all | solution.py:19
  859.2 19.5 %all_to_all.33 = bf16[32,2048,96]{1,2,0:T(8,128)(2,1)} reshape(bf16[32,8,256,96]{2,1,3,0:T(8,128)(2,1)} %copy.44) | data formatting | bytes 25165824 | tf_op jit(solution)/shard_map/all_to_all | solution.py:19
  (1 shorter events, 0.0 us)
Async XLA Ops:
  7.2 191.0 %all-reduce.3.cloned.1.call-start = ((), (), s32[]{:S(2)}) async-start(), calls=%async_computation.2 | async-start | bytes 1572864 | tf_op jit(solution)/shard_map/pmax | solution.py:10
  91.0 19.1 %copy-start = (f32[32,256,768]{1,0,2:T(8,128)S(1)}, f32[32,256,768]{1,0,2:T(8,128)}, u32[]{:S(2)}) copy-start(f32[32,256,768]{1,0,2:T(8,128)} %copy.38) | copy-start | bytes 75497472
  227.5 281.8 %copy-start.1 = (f32[256,32]{0,1:T(8,128)S(1)}, f32[256,32]{0,1:T(8,128)}, u32[]{:S(2)}) copy-start(f32[256,32]{0,1:T(8,128)} %param.10) | copy-start | bytes 98308
  227.6 281.8 %copy-start.2 = (f32[256]{0:T(256)S(1)}, f32[256]{0:T(256)}, u32[]{:S(2)}) copy-start(f32[256]{0:T(256)} %param.11) | copy-start | bytes 3076
  504.0 341.1 %all-to-all-start.1 = ((bf16[32,256,768]{1,0,2:T(8,128)(2,1)}), bf16[32,256,768]{1,0,2:T(8,128)(2,1)}, u32[]{:S(2)}, u32[]{:S(2)}) async-start(bf16[32,256,768]{1,0,2:T(8,128)(2,1)} %get-tuple-element.17), calls=%async_computation.1 | async-start | bytes 25165824 | tf_op jit(solution)/shard_map/all_to_all | solution.py:19
Sparse Core Ops, SparseCore 0:
  120.0 78.0 all-reduce.2
where the time goes:
time: 889 us; the launch traced here: 886 us
  blocking collectives  575 us (65%)
  local copies, waits for them, and re-layouts  159 us (18%)
  waiting for transfers between devices  78.2 us (9%)
  other arithmetic  53.5 us (6%)
  between operations  14.1 us (2%)
    all_gather x1, blocking collectives, on_device(): row_router = lax.all_gather(part_router, 'zero', axis=0, tiled=True)  292 us
    all_to_all x1, blocking collectives, on_device(): lax.all_to_all(narrow_gate, 'zero', split_axis=2, concat_axis=1, tiled=True)  276 us
    unnamed x13, local copies, waits for them, and re-layouts  90.9 us
    pmax x1, waiting for transfers between devices, on_device(): lax.pmax((jnp.max(jnp.abs(latest_gate), axis=1), jnp.max(jnp.abs(latest_u...  78.2 us
    all_to_all x2, local copies, waits for them, and re-layouts, on_device(): lax.all_to_all(narrow_gate, 'zero', split_axis=2, concat_axis=1, tiled=True)  33.5 us
    all_to_all x2, local copies, waits for them, and re-layouts, on_device(): lax.all_to_all(narrow_up, 'zero', split_axis=2, concat_axis=1, tiled=True)  33.5 us
    convert_element_type x1, other arithmetic, on_device(): (latest_up / jnp.expand_dims(scale_up, 1)).astype(jnp.bfloat16)  29.4 us
  transfers between devices with their start and end apart: 2, of which 1 were waited for; matrix products, arithmetic and copies ran while one was open for 2% of the time, Pallas kernels for 0%

commit v1 on v0

--- a/solution.py
+++ b/solution.py
@@ -2,6 +2,13 @@
 import jax.numpy as jnp
 from jax import lax
 from jax.sharding import PartitionSpec as P
+
+
+def stacked_exchange(x, mesh_axis, split, join):
+    size = lax.axis_size(mesh_axis)
+    blocks = jnp.stack(jnp.split(x, size, axis=split), axis=0)
+    blocks = lax.all_to_all(blocks, mesh_axis, split_axis=0, concat_axis=0)
+    return jnp.concatenate(blocks, axis=join)
 
 
 def on_device(train_gate, other_gate, train_up, other_up, router_weight, router_gain):
@@ -15,7 +22,7 @@
         (latest_up / jnp.expand_dims(scale_up, 1)).astype(jnp.bfloat16),
     )
     ready_gate, ready_up = (
-        lax.all_to_all(narrow_gate, "zero", split_axis=2, concat_axis=1, tiled=True),
+        stacked_exchange(narrow_gate, "zero", 2, 1),
         lax.all_to_all(narrow_up, "zero", split_axis=2, concat_axis=1, tiled=True),
     )
     scale_gate = lax.dynamic_slice_in_dim(

time: 889 us -> 856 us (0.963)
  blocking collectives: 575 us -> 299 us
  waiting for transfers between devices: 78.2 us -> 330 us
  local copies, waits for them, and re-layouts: 159 us -> 145 us
    all_to_all x1 -> x0, blocking collectives: 276 us -> none  [on_device(): lax.all_to_all(narrow_gate, 'zero', split_axis=2, concat_axis=1, tiled=True)]
    all_to_all x0 -> x1, waiting for transfers between devices: none -> 254 us  [stacked_exchange(): blocks = lax.all_to_all(blocks, mesh_axis, split_axis=0, concat_axis=0)]
    all_to_all x2 -> x0, local copies, waits for them, and re-layouts: 33.5 us -> none  [on_device(): lax.all_to_all(narrow_gate, 'zero', split_axis=2, concat_axis=1, tiled=True)]
    convert_element_type x0 -> x1, other arithmetic: none -> 12.9 us  [on_device(): (latest_gate / jnp.expand_dims(scale_gate, 1)).astype(jnp.bfloat16)]
    convert_element_type x1, other arithmetic: 29.4 us -> 16.9 us  [on_device(): (latest_up / jnp.expand_dims(scale_up, 1)).astype(jnp.bfloat16)]
    reshape x0 -> x1, local copies, waits for them, and re-layouts: none -> 10.9 us  [stacked_exchange(): return jnp.concatenate(blocks, axis=join)]
    unnamed x13 -> x21, local copies, waits for them, and re-layouts: 90.9 us -> 98.3 us
  transfers between devices with their start and end apart: 2 -> 3, of which waited for: 1 -> 2; matrix products, arithmetic and copies ran while one was open for 2% -> 4% of each run, Pallas kernels for 0% -> 0%
where the time goes in v1:
time: 856 us; the launch traced here: 853 us
  waiting for transfers between devices  330 us (39%)
  blocking collectives  299 us (35%)
  local copies, waits for them, and re-layouts  145 us (17%)
  other arithmetic  53.9 us (6%)
  between operations  14.1 us (2%)
  starting transfers between devices  10.9 us (1%)
    all_gather x1, blocking collectives, on_device(): row_router = lax.all_gather(part_router, 'zero', axis=0, tiled=True)  292 us
    all_to_all x1, waiting for transfers between devices, stacked_exchange(): blocks = lax.all_to_all(blocks, mesh_axis, split_axis=0, concat_axis=0)  254 us
    unnamed x21, local copies, waits for them, and re-layouts  98.3 us
    pmax x1, waiting for transfers between devices, on_device(): lax.pmax((jnp.max(jnp.abs(latest_gate), axis=1), jnp.max(jnp.abs(latest_u...  76 us
    all_to_all x2, local copies, waits for them, and re-layouts, on_device(): lax.all_to_all(narrow_up, 'zero', split_axis=2, concat_axis=1, tiled=True)  33.6 us
  transfers between devices with their start and end apart: 3, of which 2 were waited for; matrix products, arithmetic and copies ran while one was open for 4% of the time, Pallas kernels for 0%

profile of v1, /device:TPU:0, one launch (start us, length us, event | category | flops | bytes accessed | tf_op | source)
XLA Modules:
  0.0 853.4 jit_solution(17380871487517755548)
XLA Ops:
  7.2 0.0 all-reduce.3.cloned.1.call-start
  7.2 25.1 %copy.44 = f32[32,256,768]{1,0,2:T(8,128)} copy(f32[32,256,768]{2,1,0:T(8,128)} %param.8) | data formatting | bytes 50331648 | tf_op args[2]
  32.3 16.9 %copy.43 = bf16[32,256,768]{1,0,2:T(8,128)(2,1)} copy(bf16[32,256,768]{2,1,0:T(8,128)(2,1)} %param.9) | data formatting | bytes 25165824 | tf_op args[3]
  49.2 24.6 %copy.41 = f32[32,256,768]{1,2,0:T(8,128)} copy(f32[32,256,768]{2,1,0:T(8,128)} %param.6) | data formatting | bytes 50331648 | tf_op args[0]
  73.8 16.6 %copy.40 = bf16[32,256,768]{1,2,0:T(8,128)(2,1)} copy(bf16[32,256,768]{2,1,0:T(8,128)(2,1)} %param.7) | data formatting | bytes 25165824 | tf_op args[1]
  90.4 0.0 copy-start
  90.4 14.3 %abs_reduce_fusion = f32[32,768]{0,1:T(8,128)} fusion(f32[32,256,768]{1,0,2:T(8,128)} %copy.44, bf16[32,256,768]{1,0,2:T(8,128)(2,1)} %copy.43), kind=kLoop, calls=%fused_computation.1 | loop fusion | flops 25141248 | bytes 37847040 | tf_op jit(solution)/shard_map/reduce_max | solution.py:18
  104.7 4.8 copy-done
  109.5 9.7 %abs_reduce_fusion.1 = f32[32,768]{1,0:T(8,128)} fusion(f32[32,256,768]{1,2,0:T(8,128)S(1)} %copy-done, bf16[32,256,768]{1,2,0:T(8,128)(2,1)} %copy.40), kind=kLoop, calls=%fused_computation.4 | loop fusion | flops 25141248 | bytes 37847040 | tf_op jit(solution)/shard_map/reduce_max | solution.py:18
  119.2 0.0 all-reduce.3.cloned.1.call-update
  119.2 76.0 %all-reduce.3.cloned.1.call-done = (f32[32,768]{1,0:T(8,128)}, f32[32,768]{0,1:T(8,128)}) async-done(((f32[32,768]{1,0:T(8,128)}, f32[32,768]{0,1:T(8,128)}), (f32[32,768]{1,0:T(8,128)}, f32[32,768]{0,1:T(8,128)})) %all-reduce.3.cloned.1.call-update) | async-done | bytes 196624 | tf_op jit(solution)/shard_map/pmax | solution.py:17
  195.3 12.9 %divide_convert_fusion.1 = bf16[32,256,768]{1,2,0:T(8,128)(2,1)S(1)} fusion(f32[32,256,768]{1,2,0:T(8,128)} %copy.41, bf16[32,256,768]{1,2,0:T(8,128)(2,1)} %copy.40, f32[32,768]{1,0:T(8,128)} %get-tuple-element.20), kind=kLoop, calls=%fused_computation.3 | loop fusion | flops 25165824 | bytes 50429952 | tf_op jit(solution)/shard_map/convert_element_type | solution.py:21
  208.1 1.2 fusion.7
  209.4 1.2 fusion.6
  210.6 1.2 fusion.5
  211.9 1.2 fusion.4
  213.1 1.2 fusion.3
  214.4 1.2 fusion.2
  215.6 1.2 fusion.1
  216.8 1.2 fusion
  218.1 0.0 copy-start.1
  218.1 5.5 all-to-all-start
  223.6 0.0 copy-done.1
  223.7 16.9 %divide_convert_fusion = bf16[32,256,768]{1,0,2:T(8,128)(2,1)} fusion(f32[32,256,768]{1,0,2:T(8,128)} %copy.44, bf16[32,256,768]{1,0,2:T(8,128)(2,1)} %copy.43, f32[32,768]{0,1:T(8,128)S(1)} %copy-done.1), kind=kLoop, calls=%fused_computation | loop fusion | flops 25165824 | bytes 50429952 | tf_op jit(solution)/shard_map/convert_element_type | solution.py:22
  240.6 0.0 copy-start.2
  240.6 0.0 copy-start.3
  240.6 254.3 %all-to-all-done = bf16[8,32,256,96]{2,3,1,0:T(8,128)(2,1)} async-done(((bf16[8,32,256,96]{2,3,1,0:T(8,128)(2,1)}), bf16[8,32,256,96]{2,3,1,0:T(8,128)(2,1)}, u32[]{:S(2)}, u32[]{:S(2)}) %all-to-all-start) | async-done | bytes 12582944 | tf_op jit(solution)/shard_map/all_to_all | solution.py:10
  494.9 5.4 all-to-all-start.1
  500.3 0.0 copy-done.2
  500.3 0.0 copy-done.3
  500.3 291.6 %all_gather.6 = bf16[2048,32]{0,1:T(8,128)(2,1)S(1)} all-gather(bf16[256,32]{0,1:T(8,128)(2,1)S(1)} %multiply_convert_fusion), channel_id=1, replica_groups=mesh['bank'=4,'zero'=8] {'zero'}, dimensions={0}, use_global_device_ids=true | all-gather | bytes 147456 | tf_op jit(solution)/shard_map/all_gather | solution.py:35
  791.9 7.1 all_gather.7
  799.0 1.0 copy.48
  800.1 0.7 copy.47
  800.7 1.4 constant_dynamic-slice_fusion.1
  802.2 10.9 %copy.50 = bf16[8,32,12,8,256]{4,3,0,2,1:T(8,128)(2,1)} copy(bf16[8,32,12,8,256]{4,3,2,1,0:T(8,128)(2,1)} %bitcast.12) | data formatting | bytes 25165824 | tf_op jit(solution)/shard_map/reshape | solution.py:11
  813.0 0.0 all-to-all-done.1
  813.0 14.1 %copy.46 = bf16[32,8,256,96]{2,1,3,0:T(8,128)(2,1)} copy(bf16[32,8,256,96]{2,0,3,1:T(8,128)(2,1)} %bitcast.11) | data formatting | bytes 25165824 | tf_op jit(solution)/shard_map/all_to_all | solution.py:26
  827.1 19.5 %all_to_all.20 = bf16[32,2048,96]{1,2,0:T(8,128)(2,1)} reshape(bf16[32,8,256,96]{2,1,3,0:T(8,128)(2,1)} %copy.46) | data formatting | bytes 25165824 | tf_op jit(solution)/shard_map/all_to_all | solution.py:26
  (2 shorter events, 0.0 us)
Async XLA Ops:
  7.2 188.1 %all-reduce.3.cloned.1.call-start = ((), (), s32[]{:S(2)}) async-start(), calls=%async_computation.2 | async-start | bytes 983040 | tf_op jit(solution)/shard_map/pmax | solution.py:17
  90.4 19.1 %copy-start = (f32[32,256,768]{1,2,0:T(8,128)S(1)}, f32[32,256,768]{1,2,0:T(8,128)}, u32[]{:S(2)}) copy-start(f32[32,256,768]{1,2,0:T(8,128)} %copy.41) | copy-start | bytes 75497472
  218.1 5.6 copy-start.1
  218.1 276.8 %all-to-all-start = ((bf16[8,32,256,96]{2,3,1,0:T(8,128)(2,1)}), bf16[8,32,256,96]{2,3,1,0:T(8,128)(2,1)}, u32[]{:S(2)}, u32[]{:S(2)}) async-start(bf16[8,32,256,96]{2,3,1,0:T(8,128)(2,1)} %fusion), calls=%async_computation | async-start | bytes 25165824 | tf_op jit(solution)/shard_map/all_to_all | solution.py:10
  240.6 259.7 %copy-start.2 = (f32[256,32]{0,1:T(8,128)S(1)}, f32[256,32]{0,1:T(8,128)}, u32[]{:S(2)}) copy-start(f32[256,32]{0,1:T(8,128)} %param.10) | copy-start | bytes 98308
  240.6 259.7 %copy-start.3 = (f32[256]{0:T(256)S(1)}, f32[256]{0:T(256)}, u32[]{:S(2)}) copy-start(f32[256]{0:T(256)} %param.11) | copy-start | bytes 3076
  494.9 318.1 %all-to-all-start.1 = ((bf16[32,256,768]{1,0,2:T(8,128)(2,1)}), bf16[32,256,768]{1,0,2:T(8,128)(2,1)}, u32[]{:S(2)}, u32[]{:S(2)}) async-start(bf16[32,256,768]{1,0,2:T(8,128)(2,1)} %divide_convert_fusion), calls=%async_computation.1 | async-start | bytes 25165824 | tf_op jit(solution)/shard_map/all_to_all | solution.py:26
Sparse Core Ops, SparseCore 0:
  119.4 75.8 all-reduce.2

commit v2 on v0

--- a/solution.py
+++ b/solution.py
@@ -26,7 +26,8 @@
     )
     part_router = (router_weight * router_gain[:, None]).astype(jnp.bfloat16)
     row_router = lax.all_gather(part_router, "zero", axis=0, tiled=True)
-    serve_router = lax.all_gather(row_router, "bank", axis=1, tiled=True)
+    parts = lax.all_gather(row_router, "bank", axis=0, tiled=False)
+    serve_router = jnp.concatenate(parts, axis=1)
     return (ready_gate, ready_up, scale_gate, scale_up, serve_router)
 
 

time: 889 us -> 889 us (level)
  no operation moved by 1% of the time
where the time goes in v2:
time: 889 us; the launch traced here: 886 us
  blocking collectives  575 us (65%)
  local copies, waits for them, and re-layouts  160 us (18%)
  waiting for transfers between devices  78.2 us (9%)
  other arithmetic  53.5 us (6%)
  between operations  14.1 us (2%)
    all_gather x1, blocking collectives, on_device(): row_router = lax.all_gather(part_router, 'zero', axis=0, tiled=True)  292 us
    all_to_all x1, blocking collectives, on_device(): lax.all_to_all(narrow_gate, 'zero', split_axis=2, concat_axis=1, tiled=True)  276 us
    unnamed x13, local copies, waits for them, and re-layouts  90.9 us
    pmax x1, waiting for transfers between devices, on_device(): lax.pmax((jnp.max(jnp.abs(latest_gate), axis=1), jnp.max(jnp.abs(latest_u...  78.2 us
    all_to_all x2, local copies, waits for them, and re-layouts, on_device(): lax.all_to_all(narrow_gate, 'zero', split_axis=2, concat_axis=1, tiled=True)  33.5 us
    all_to_all x2, local copies, waits for them, and re-layouts, on_device(): lax.all_to_all(narrow_up, 'zero', split_axis=2, concat_axis=1, tiled=True)  33.5 us
    convert_element_type x1, other arithmetic, on_device(): (latest_up / jnp.expand_dims(scale_up, 1)).astype(jnp.bfloat16)  29.4 us
  transfers between devices with their start and end apart: 2, of which 1 were waited for; matrix products, arithmetic and copies ran while one was open for 2% of the time, Pallas kernels for 0%

profile of v2, /device:TPU:0, one launch (start us, length us, event | category | flops | bytes accessed | tf_op | source)
XLA Modules:
  0.0 886.2 jit_solution(148892652662324902)
XLA Ops:
  7.2 0.0 all-reduce.3.cloned.1.call-start
  7.2 25.0 %copy.44 = f32[32,256,768]{1,0,2:T(8,128)} copy(f32[32,256,768]{2,1,0:T(8,128)} %param.8) | data formatting | bytes 50331648 | tf_op args[2]
  32.2 16.9 %copy.43 = bf16[32,256,768]{1,0,2:T(8,128)(2,1)} copy(bf16[32,256,768]{2,1,0:T(8,128)(2,1)} %param.9) | data formatting | bytes 25165824 | tf_op args[3]
  49.1 25.0 %copy.40 = f32[32,256,768]{1,0,2:T(8,128)} copy(f32[32,256,768]{2,1,0:T(8,128)} %param.6) | data formatting | bytes 50331648 | tf_op args[0]
  74.2 16.9 %copy.39 = bf16[32,256,768]{1,0,2:T(8,128)(2,1)} copy(bf16[32,256,768]{2,1,0:T(8,128)(2,1)} %param.7) | data formatting | bytes 25165824 | tf_op args[1]
  91.0 0.0 copy-start
  91.0 14.4 %abs_reduce_fusion = f32[32,768]{0,1:T(8,128)} fusion(f32[32,256,768]{1,0,2:T(8,128)} %copy.44, bf16[32,256,768]{1,0,2:T(8,128)(2,1)} %copy.43), kind=kLoop, calls=%fused_computation.1 | loop fusion | flops 25141248 | bytes 37847040 | tf_op jit(solution)/shard_map/reduce_max | solution.py:11
  105.4 4.7 copy-done
  110.1 9.7 %abs_reduce_fusion.1 = f32[32,768]{0,1:T(8,128)} fusion(f32[32,256,768]{1,0,2:T(8,128)S(1)} %copy-done, bf16[32,256,768]{1,0,2:T(8,128)(2,1)} %copy.39), kind=kLoop, calls=%fused_computation.4 | loop fusion | flops 25141248 | bytes 37847040 | tf_op jit(solution)/shard_map/reduce_max | solution.py:11
  119.9 0.0 all-reduce.3.cloned.1.call-update
  119.9 78.2 %all-reduce.3.cloned.1.call-done = (f32[32,768]{0,1:T(8,128)}, f32[32,768]{0,1:T(8,128)}) async-done(((f32[32,768]{0,1:T(8,128)}, f32[32,768]{0,1:T(8,128)}), (f32[32,768]{0,1:T(8,128)}, f32[32,768]{0,1:T(8,128)})) %all-reduce.3.cloned.1.call-update) | async-done | bytes 196624 | tf_op jit(solution)/shard_map/pmax | solution.py:10
  198.1 29.4 %divide_convert_fusion = (bf16[32,256,768]{1,0,2:T(8,128)(2,1)}, bf16[32,256,768]{1,0,2:T(8,128)(2,1)S(1)}) fusion(f32[32,256,768]{1,0,2:T(8,128)} %copy.44, bf16[32,256,768]{1,0,2:T(8,128)(2,1)} %copy.43, f32[32,768]{0,1:T(8,128)} %get-tuple-element.26, f32[32,768]{0,1:T(8,128)} %get-tuple-element.25, f32[32,256,768]{1,0,2:T(8,128)} %copy.40, ...), kind=kLoop, calls=%fused_computation | loop fusion | flops 50331648 | bytes 100859904 | tf_op jit(solution)/shard_map/convert_element_type | solution.py:15
  227.5 0.0 copy-start.1
  227.6 0.0 copy-start.2
  227.6 276.4 %all_to_all.36 = bf16[32,256,768]{1,0,2:T(8,128)(2,1)} all-to-all(bf16[32,256,768]{1,0,2:T(8,128)(2,1)S(1)} %get-tuple-element.28), channel_id=1, replica_groups=mesh['bank'=4,'zero'=8] {'zero'}, dimensions={2} | all-to-all | bytes 25165824 | tf_op jit(solution)/shard_map/all_to_all | solution.py:18
  504.0 5.4 all-to-all-start.1
  509.3 0.0 copy-done.1
  509.4 0.0 copy-done.2
  509.4 292.0 %all_gather.9 = bf16[2048,32]{0,1:T(8,128)(2,1)S(1)} all-gather(bf16[256,32]{0,1:T(8,128)(2,1)S(1)} %multiply_convert_fusion), channel_id=1, replica_groups=mesh['bank'=4,'zero'=8] {'zero'}, dimensions={0}, use_global_device_ids=true | all-gather | bytes 147456 | tf_op jit(solution)/shard_map/all_gather | solution.py:28
  801.4 7.0 all-gather
  808.4 0.4 reshape.21
  808.8 0.3 copy.47
  809.1 1.0 copy.50
  810.1 0.8 constant_dynamic-slice_fusion
  810.9 0.7 copy.48
  811.6 0.7 copy.49
  812.3 14.1 %copy.42 = bf16[32,8,256,96]{2,1,3,0:T(8,128)(2,1)} copy(bf16[32,8,256,96]{2,0,3,1:T(8,128)(2,1)} %bitcast.18) | data formatting | bytes 25165824 | tf_op jit(solution)/shard_map/all_to_all | solution.py:18
  826.3 19.5 %all_to_all.29 = bf16[32,2048,96]{1,2,0:T(8,128)(2,1)} reshape(bf16[32,8,256,96]{2,1,3,0:T(8,128)(2,1)} %copy.42) | data formatting | bytes 25165824 | tf_op jit(solution)/shard_map/all_to_all | solution.py:18
  845.8 0.0 all-to-all-done.1
  845.8 14.1 %copy.46 = bf16[32,8,256,96]{2,1,3,0:T(8,128)(2,1)} copy(bf16[32,8,256,96]{2,0,3,1:T(8,128)(2,1)} %bitcast.5) | data formatting | bytes 25165824 | tf_op jit(solution)/shard_map/all_to_all | solution.py:19
  859.9 19.5 %all_to_all.33 = bf16[32,2048,96]{1,2,0:T(8,128)(2,1)} reshape(bf16[32,8,256,96]{2,1,3,0:T(8,128)(2,1)} %copy.46) | data formatting | bytes 25165824 | tf_op jit(solution)/shard_map/all_to_all | solution.py:19
  (1 shorter events, 0.0 us)
Async XLA Ops:
  7.2 191.0 %all-reduce.3.cloned.1.call-start = ((), (), s32[]{:S(2)}) async-start(), calls=%async_computation.2 | async-start | bytes 1572864 | tf_op jit(solution)/shard_map/pmax | solution.py:10
  91.0 19.1 %copy-start = (f32[32,256,768]{1,0,2:T(8,128)S(1)}, f32[32,256,768]{1,0,2:T(8,128)}, u32[]{:S(2)}) copy-start(f32[32,256,768]{1,0,2:T(8,128)} %copy.40) | copy-start | bytes 75497472
  227.5 281.8 %copy-start.1 = (f32[256,32]{0,1:T(8,128)S(1)}, f32[256,32]{0,1:T(8,128)}, u32[]{:S(2)}) copy-start(f32[256,32]{0,1:T(8,128)} %param.10) | copy-start | bytes 98308
  227.6 281.8 %copy-start.2 = (f32[256]{0:T(256)S(1)}, f32[256]{0:T(256)}, u32[]{:S(2)}) copy-start(f32[256]{0:T(256)} %param.11) | copy-start | bytes 3076
  504.0 341.8 %all-to-all-start.1 = ((bf16[32,256,768]{1,0,2:T(8,128)(2,1)}), bf16[32,256,768]{1,0,2:T(8,128)(2,1)}, u32[]{:S(2)}, u32[]{:S(2)}) async-start(bf16[32,256,768]{1,0,2:T(8,128)(2,1)} %get-tuple-element.27), calls=%async_computation.1 | async-start | bytes 25165824 | tf_op jit(solution)/shard_map/all_to_all | solution.py:19
Sparse Core Ops, SparseCore 0:
  120.0 78.0 all-reduce.2
